TPU v7x, 512 devices: a whole 4x8x8 slice. The times are simulated.
512 devices in a mesh: fsdp: 64 (over x, y, core), dp: 8 (over z).
Axes of the slice: x: 4, y: 8, z: 8, core: 2. Of those that a mesh axis runs over, the one named last changes fastest.
Arguments:
- grads: bfloat16 [8, 1024, 28672], P('dp', 'fsdp')
- block_slot: int32 [28], replicated, may hold values from 0 to 63, as said below
- left_stats: float32 [64, 1024, 1024], P('fsdp', 'dp')
- right_stats: float32 [64, 1024, 1024], P('fsdp', 'dp')
- left_root: bfloat16 [64, 1024, 1024], P('fsdp', 'dp')
- right_root: bfloat16 [64, 1024, 1024], P('fsdp', 'dp')
Outputs:
- left_new: float32 [64, 1024, 1024], P('fsdp', 'dp')
- right_new: float32 [64, 1024, 1024], P('fsdp', 'dp')
- update: bfloat16 [1024, 28672], P('fsdp')
Inputs may be any that keep to these rules, and one draw needn't show every extreme that they name: The entries of block_slot are distinct. Block b's statistics and roots sit in slot block_slot[b], which belongs to the fsdp device of index block_slot[b]; slots that no block names are empty and their statistics pass through unchanged.
All inputs are finite; a program needn't handle non-finite values.
Results may differ from a plain program's by a relative error of at most 0.015.
Values may be sent and summed in bfloat16 or wider, within the bound.
No kernel may reach another device: no remote copies, remote signals or barrier semaphores. Data moves between devices by JAX's collectives and lax.ppermute only.
A program may use at most 64 MiB of HBM per device.

v0:
```python
import jax
import jax.numpy as jnp
from jax import lax
from jax.sharding import Mesh
from jax.sharding import PartitionSpec as P

FSDP = ("fsdp_0", "fsdp_1", "fsdp_2")
epsilon = 1e-06


def split_terms(value):
    high = lax.reduce_precision(value, 8, 7)
    middle = lax.reduce_precision(value - high, 8, 7)
    low = value - high - middle
    return [term.astype(jnp.bfloat16) for term in (high, middle, low)]


def per_device(grads, block_slot, left_stats, right_stats, left_root, right_root):
    rows = grads[0]
    row_dev, col_count = rows.shape
    block_size = left_stats.shape[2]
    block_count = col_count // block_size
    shared = left_stats.shape[1]
    replicas = lax.axis_size("dp")
    total_slots = lax.axis_size(FSDP)
    slot_ids = jnp.arange(total_slots, dtype=jnp.int32)
    matches = block_slot[None, :] == slot_ids[:, None]
    filled = jnp.any(matches, axis=1)
    numbers = jnp.arange(block_count, dtype=jnp.int32)
    source = jnp.sum(jnp.where(matches, numbers[None, :], 0), axis=1)
    whole_left = lax.all_gather(left_root[0], "dp", axis=0, tiled=True)
    shares = rows.reshape(row_dev, block_count, replicas, shared).transpose(2, 1, 0, 3)
    shares = shares.reshape(replicas, block_count * row_dev, shared)
    roots = right_root[0].reshape(shared, replicas, shared).transpose(1, 0, 2)
    message = jnp.concatenate([shares, roots], axis=1)
    received = lax.all_to_all(message, "dp", 0, 0, tiled=True)
    summed = jnp.sum(received[:, : block_count * row_dev].astype(jnp.float32), axis=0)
    summed = summed.astype(jnp.bfloat16).reshape(block_count, row_dev, shared)
    right_cols = received[:, block_count * row_dev :]
    outgoing = jnp.where(
        filled[:, None, None], jnp.take(summed, source, axis=0), jnp.zeros((), jnp.bfloat16)
    )
    incoming = lax.all_to_all(outgoing, FSDP, 0, 0, tiled=True)
    mine, whole_left = lax.optimization_barrier((incoming.reshape(block_size, shared), whole_left))
    gradient = lax.all_gather(mine, "dp", axis=1, tiled=True)
    inner = jnp.einsum(
        "rk,kc->rc",
        gradient,
        right_cols.reshape(block_size, shared),
        preferred_element_type=jnp.float32,
    )
    high = lax.reduce_precision(inner, 8, 7)
    low = (inner - high).astype(jnp.bfloat16)
    high = high.astype(jnp.bfloat16)
    both = jnp.einsum(
        "kr,rc->kc", whole_left, high, preferred_element_type=jnp.float32
    ) + jnp.einsum("kr,rc->kc", whole_left, low, preferred_element_type=jnp.float32)
    partial = split_terms(jnp.sum(both * both))
    lanes = jnp.concatenate([jnp.stack(partial), jnp.zeros(shared - 3, jnp.bfloat16)])
    marks = jnp.broadcast_to(lanes[None, None, :], (total_slots, 8, shared))
    both = both.astype(jnp.bfloat16).reshape(total_slots, row_dev, shared)
    back = lax.all_to_all(jnp.concatenate([both, marks], axis=1), FSDP, 0, 0, tiled=True)
    row_start = lax.axis_index("dp") * shared
    own_rows = lax.dynamic_slice_in_dim(gradient, row_start, shared, 0)
    left_new = left_stats + jnp.einsum(
        "rc,kc->rk", own_rows, gradient, preferred_element_type=jnp.float32
    )
    right_new = right_stats + jnp.einsum(
        "rc,rk->ck", mine, gradient, preferred_element_type=jnp.float32
    )
    picked = jnp.take(back, block_slot, axis=0)
    terms = jnp.zeros((32, shared), jnp.bfloat16).at[:block_count].set(picked[:, row_dev, :])
    tiles = picked[:, :row_dev].reshape(block_count * row_dev, shared)
    gathered = lax.all_gather(jnp.concatenate([tiles, terms]), "dp", axis=0, tiled=False)
    full = gathered[:, : block_count * row_dev].reshape(replicas, block_count, row_dev, shared)
    terms = gathered[:, block_count * row_dev :][:, :block_count, :3].astype(jnp.float32)
    squares = jnp.sum(terms, axis=(0, 2))
    factor = lax.rsqrt(squares / (block_size * block_size) + epsilon)
    update = (full.astype(jnp.float32) * factor[None, :, None, None]).astype(jnp.bfloat16)
    update = update.transpose(2, 1, 0, 3).reshape(row_dev, col_count)
    return (left_new, right_new, update)


def solution(mesh):
    split = Mesh(
        mesh.devices.reshape(4, 8, 2, mesh.shape["dp"]), ("fsdp_0", "fsdp_1", "fsdp_2", "dp")
    )
    placed = (
        P("dp", FSDP, None),
        P(),
        P(FSDP, "dp", None),
        P(FSDP, "dp", None),
        P(FSDP, "dp", None),
        P(FSDP, "dp", None),
    )
    return jax.shard_map(
        per_device,
        mesh=split,
        in_specs=placed,
        out_specs=(P(FSDP, "dp", None), P(FSDP, "dp", None), P(FSDP, None)),
        check_vma=False,
    )
```

profile of v0, /device:TPU:8, one launch (start us, length us, event | category | flops | bytes accessed | tf_op | source)
XLA Modules:
  0.0 203.1 jit_solution(17511728519001342608)
XLA Ops:
  7.2 0.0 all-gather.7.cloned.1.call-start
  7.2 0.7 all-gather.7.cloned.1.call-update
  7.9 1.1 copy.15
  9.0 0.2 copy.16
  9.2 1.3 copy.19
  10.5 0.4 copy.14
  10.9 0.0 copy-start.6
  10.9 1.1 pad_maximum_fusion
  12.0 10.3 %all-to-all-start = ((bf16[8,576,128]{2,1,0:T(8,128)(2,1)}), bf16[8,576,128]{2,1,0:T(8,128)(2,1)S(1)}, u32[]{:S(2)}, u32[]{:S(2)}) async-start(bf16[8,576,128]{2,1,0:T(8,128)(2,1)} %pad_maximum_fusion), calls=%async_computation | async-start | bytes 2359296 | tf_op jit(solution)/shard_map/all_to_all | solution.py:36
  22.3 0.0 all-gather.5.cloned.1.call-start
  22.4 0.0 copy-done.6
  22.4 0.1 select_reduce_fusion
  22.5 0.1 fusion.10
  22.6 42.0 %all-to-all-done = bf16[8,576,128]{2,1,0:T(8,128)(2,1)S(1)} async-done(((bf16[8,576,128]{2,1,0:T(8,128)(2,1)}), bf16[8,576,128]{2,1,0:T(8,128)(2,1)S(1)}, u32[]{:S(2)}, u32[]{:S(2)}) %all-to-all-start) | async-done | bytes 1179680 | tf_op jit(solution)/shard_map/all_to_all | solution.py:36
  64.5 0.1 slice_reduce_fusion
  64.7 0.6 gather_fusion
  65.3 0.2 select_select_fusion
  65.5 22.5 %all_to_all.15 = bf16[64,16,128]{2,1,0:T(8,128)(2,1)} all-to-all(bf16[64,16,128]{2,1,0:T(8,128)(2,1)S(1)} %select_select_fusion), channel_id=1, replica_groups=mesh['fsdp_0'=4,'fsdp_1'=8,'fsdp_2'=2,'dp'=8] {'fsdp_0','fsdp_1','fsdp_2'}, dimensions={0} | all-to-all | bytes 524288 | tf_op jit(solution)/shard_map/all_to_all | solution.py:43
  88.0 0.0 all-gather.7.cloned.1.call-done
  88.0 0.0 copy-start.1
  88.0 0.0 all-gather.5.cloned.1.call-update
  88.0 42.6 %all-gather.5.cloned.1.call-done = bf16[1024,1024]{1,0:T(8,128)(2,1)} async-done(((bf16[1024,128]{1,0:T(8,128)(2,1)}), bf16[1024,1024]{1,0:T(8,128)(2,1)}) %all-gather.5.cloned.1.call-update) | async-done | bytes 2097168 | tf_op jit(solution)/shard_map/all_gather | solution.py:45
  130.7 2.3 %fusion.14 = f32[1024,128]{1,0:T(8,128)S(1)} fusion(bf16[1024,1024]{1,0:T(8,128)(2,1)} %all-gather.5.cloned.1.call-done, bf16[1024,128]{1,0:T(8,128)(2,1)S(1)} %bitcast.64), kind=kOutput, calls=%fused_computation.42 | convolution fusion | flops 268435456 | bytes 2883584 | tf_op jit(solution)/shard_map/rk,kc->rc/dot_general | solution.py:46
  133.0 0.0 copy-done.1
  133.0 0.0 copy-start.2
  133.0 0.7 fusion.6
  133.7 0.9 copy-done.2
  134.6 0.0 copy-start
  134.6 0.0 copy-start.4
  134.6 1.3 fusion.13
  140.8 0.1 pad_maximum_fusion.2
  140.9 0.8 pad_maximum_fusion.1
  141.7 0.0 copy-start.3
  141.7 10.4 %all-to-all-start.2 = ((bf16[64,24,128]{2,1,0:T(8,128)(2,1)}), bf16[64,24,128]{2,1,0:T(8,128)(2,1)S(1)}, u32[]{:S(2)}, u32[]{:S(2)}) async-start(bf16[64,24,128]{2,1,0:T(8,128)(2,1)} %pad_maximum_fusion.1), calls=%async_computation.2 | async-start | bytes 786432 | tf_op jit(solution)/shard_map/all_to_all | solution.py:62
  152.1 0.0 copy-start.5
  152.1 0.0 copy-done
  152.2 0.0 copy-done.4
  152.2 1.6 fusion.1
  153.8 0.0 copy-done.3
  153.8 0.0 copy-done.5
  153.8 1.3 fusion.2
  155.1 11.5 %all-to-all-done.2 = bf16[64,24,128]{2,1,0:T(8,128)(2,1)S(1)} async-done(((bf16[64,24,128]{2,1,0:T(8,128)(2,1)}), bf16[64,24,128]{2,1,0:T(8,128)(2,1)S(1)}, u32[]{:S(2)}, u32[]{:S(2)}) %all-to-all-start.2) | async-done | bytes 393248 | tf_op jit(solution)/shard_map/all_to_all | solution.py:62
  166.5 0.6 gather_fusion.1
  167.1 0.1 broadcast_select_fusion
  167.3 26.6 %all-gather.1 = bf16[3840,128]{1,0:T(8,128)(2,1)S(1)} all-gather(bf16[480,128]{1,0:T(8,128)(2,1)S(1)} %fusion.9), channel_id=3, replica_groups=mesh['fsdp_0'=4,'fsdp_1'=8,'fsdp_2'=2,'dp'=8] {'dp'}, dimensions={0}, use_global_device_ids=true | all-gather | bytes 1105920 | tf_op jit(solution)/shard_map/all_gather | solution.py:74
  193.9 0.1 convert_reduce_fusion
  194.1 0.1 slice.50
  194.2 0.3 fusion.3
  194.4 0.6 copy.17
  195.0 1.3 copy.23
  (14 shorter events, 0.1 us)
Async XLA Ops:
  7.2 80.8 %all-gather.7.cloned.1.call-start = ((), (), s32[]{:S(2)}) async-start(), calls=%async_computation.4 | async-start | bytes 2359296 | tf_op jit(solution)/shard_map/all_gather | solution.py:31
  10.9 11.5 %copy-start.6 = (s32[28]{0:T(128)S(1)}, s32[28]{0:T(128)}, u32[]{:S(2)}) copy-start(s32[28]{0:T(128)} %param.9) | copy-start | bytes 340
  12.0 52.5 %all-to-all-start = ((bf16[8,576,128]{2,1,0:T(8,128)(2,1)}), bf16[8,576,128]{2,1,0:T(8,128)(2,1)S(1)}, u32[]{:S(2)}, u32[]{:S(2)}) async-start(bf16[8,576,128]{2,1,0:T(8,128)(2,1)} %pad_maximum_fusion), calls=%async_computation | async-start | bytes 2359296 | tf_op jit(solution)/shard_map/all_to_all | solution.py:36
  22.3 108.3 %all-gather.5.cloned.1.call-start = ((), (), s32[]{:S(2)}) async-start(), calls=%async_computation.3 | async-start | bytes 2359296 | tf_op jit(solution)/shard_map/all_gather | solution.py:45
  88.0 45.0 %copy-start.1 = (bf16[1,1024,1024]{2,1,0:T(8,128)(2,1)S(1)}, bf16[1,1024,1024]{2,1,0:T(8,128)(2,1)}, u32[]{:S(2)}) copy-start(bf16[1,1024,1024]{2,1,0:T(8,128)(2,1)} %all-gather.7.cloned.1.call-done) | copy-start | bytes 6291460
  133.0 1.6 copy-start.2
  134.6 17.6 %copy-start = (bf16[1024,1024]{1,0:T(8,128)(2,1)S(1)}, bf16[1024,1024]{1,0:T(8,128)(2,1)}, u32[]{:S(2)}) copy-start(bf16[1024,1024]{1,0:T(8,128)(2,1)} %all-gather.5.cloned.1.call-done) | copy-start | bytes 6291460
  134.6 17.6 %copy-start.4 = (f32[1,128,1024]{2,1,0:T(8,128)S(1)}, f32[1,128,1024]{2,1,0:T(8,128)}, u32[]{:S(2)}) copy-start(f32[1,128,1024]{2,1,0:T(8,128)} %param.10) | copy-start | bytes 1572868
  141.7 12.1 %copy-start.3 = (bf16[64,16,128]{2,1,0:T(8,128)(2,1)S(1)}, bf16[64,16,128]{2,1,0:T(8,128)(2,1)}, u32[]{:S(2)}) copy-start(bf16[64,16,128]{2,1,0:T(8,128)(2,1)} %all_to_all.15) | copy-start | bytes 786436
  141.7 24.8 %all-to-all-start.2 = ((bf16[64,24,128]{2,1,0:T(8,128)(2,1)}), bf16[64,24,128]{2,1,0:T(8,128)(2,1)S(1)}, u32[]{:S(2)}, u32[]{:S(2)}) async-start(bf16[64,24,128]{2,1,0:T(8,128)(2,1)} %pad_maximum_fusion.1), calls=%async_computation.2 | async-start | bytes 786432 | tf_op jit(solution)/shard_map/all_to_all | solution.py:62
  152.1 1.7 copy-start.5
Sparse Core Ops, SparseCore 0:
  10.1 64.5 all-gather.6
  88.1 42.4 all-gather.4
where the time goes:
time: 204 us; the launch traced here: 203 us
  waiting for transfers between devices  96.7 us (47%)
  blocking collectives  49.1 us (24%)
  starting transfers between devices  20.8 us (10%)
  between operations  19.2 us (9%)
  matrix products  7.21 us (4%)
  local copies, waits for them, and re-layouts  7.09 us (3%)
  other arithmetic  3.03 us (1%)
    all_gather x1, waiting for transfers between devices, per_device(): gradient = lax.all_gather(mine, 'dp', axis=1, tiled=True)  42.6 us
    all_to_all x1, waiting for transfers between devices, per_device(): received = lax.all_to_all(message, 'dp', 0, 0, tiled=True)  42 us
    all_gather x1, blocking collectives, per_device(): lax.all_gather(jnp.concatenate([tiles, terms]), 'dp', axis=0, tiled=False)  26.6 us
    all_to_all x1, blocking collectives, per_device(): incoming = lax.all_to_all(outgoing, FSDP, 0, 0, tiled=True)  22.5 us
    all_to_all x1, waiting for transfers between devices, per_device(): lax.all_to_all(jnp.concatenate([both, marks], axis=1), FSDP, 0, 0, tiled=...  11.5 us
    all_to_all x1, starting transfers between devices, per_device(): lax.all_to_all(jnp.concatenate([both, marks], axis=1), FSDP, 0, 0, tiled=...  10.4 us
    all_to_all x1, starting transfers between devices, per_device(): received = lax.all_to_all(message, 'dp', 0, 0, tiled=True)  10.3 us
    unnamed x18, local copies, waits for them, and re-layouts  4.61 us
  transfers between devices with their start and end apart: 4, of which 3 were waited for; matrix products, arithmetic and copies ran while one was open for 4% of the time, Pallas kernels for 0%

commit v1 on v0

--- a/solution.py
+++ b/solution.py
@@ -42,7 +42,16 @@
     )
     incoming = lax.all_to_all(outgoing, FSDP, 0, 0, tiled=True)
     mine, whole_left = lax.optimization_barrier((incoming.reshape(block_size, shared), whole_left))
-    gradient = lax.all_gather(mine, "dp", axis=1, tiled=True)
+
+    def loops_point(row_data):
+        axis_n = lax.axis_size("dp")
+        x_next = range(row_data.ndim)
+        front = map(lambda j0: axis_n if j0 == 1 else 1, x_next)
+        passed = list(front)
+        built = jnp.tile(row_data, passed)
+        return lax.all_to_all(built, "dp", split_axis=1, concat_axis=1, tiled=True)
+
+    gradient = loops_point(mine)
     inner = jnp.einsum(
         "rk,kc->rc",
         gradient,

time: 204 us -> 210 us (1.029)
  waiting for transfers between devices: 96.7 us -> 100 us
  local copies, waits for them, and re-layouts: 7.09 us -> 10.3 us
    all_to_all x0 -> x1, waiting for transfers between devices: none -> 51.8 us  [loops_point(): return lax.all_to_all(built, 'dp', split_axis=1, concat_axis=1, tiled=True)]
    all_gather x1 -> x0, waiting for transfers between devices: 42.6 us -> none  [per_device(): gradient = lax.all_gather(mine, 'dp', axis=1, tiled=True)]
    all_to_all x1, waiting for transfers between devices: 11.5 us -> 7.02 us  [per_device(): lax.all_to_all(jnp.concatenate([both, marks], axis=1), FSDP, 0, 0, tiled=...]
    all_to_all x1, starting transfers between devices: 10.4 us -> 6.03 us  [per_device(): lax.all_to_all(jnp.concatenate([both, marks], axis=1), FSDP, 0, 0, tiled=...]
    all_to_all x0 -> x1, starting transfers between devices: none -> 3.6 us  [loops_point(): return lax.all_to_all(built, 'dp', split_axis=1, concat_axis=1, tiled=True)]
    all_to_all x0 -> x1, local copies, waits for them, and re-layouts: none -> 2.61 us  [loops_point(): return lax.all_to_all(built, 'dp', split_axis=1, concat_axis=1, tiled=True)]
    unnamed x18 -> x16, local copies, waits for them, and re-layouts: 4.61 us -> 3.66 us
  transfers between devices with their start and end apart: 4 -> 4, of which waited for: 3 -> 3; matrix products, arithmetic and copies ran while one was open for 4% -> 6% of each run, Pallas kernels for 0% -> 0%
where the time goes in v1:
time: 210 us; the launch traced here: 209 us
  waiting for transfers between devices  100 us (48%)
  blocking collectives  49 us (23%)
  starting transfers between devices  20 us (10%)
  between operations  19.2 us (9%)
  local copies, waits for them, and re-layouts  10.3 us (5%)
  matrix products  7.46 us (4%)
  other arithmetic  3.03 us (1%)
    all_to_all x1, waiting for transfers between devices, loops_point(): return lax.all_to_all(built, 'dp', split_axis=1, concat_axis=1, tiled=True)  51.8 us
    all_to_all x1, waiting for transfers between devices, per_device(): received = lax.all_to_all(message, 'dp', 0, 0, tiled=True)  41 us
    all_gather x1, blocking collectives, per_device(): lax.all_gather(jnp.concatenate([tiles, terms]), 'dp', axis=0, tiled=False)  26.6 us
    all_to_all x1, blocking collectives, per_device(): incoming = lax.all_to_all(outgoing, FSDP, 0, 0, tiled=True)  22.4 us
    all_to_all x1, starting transfers between devices, per_device(): received = lax.all_to_all(message, 'dp', 0, 0, tiled=True)  10.3 us
    all_to_all x1, waiting for transfers between devices, per_device(): lax.all_to_all(jnp.concatenate([both, marks], axis=1), FSDP, 0, 0, tiled=...  7.02 us
    all_to_all x1, starting transfers between devices, per_device(): lax.all_to_all(jnp.concatenate([both, marks], axis=1), FSDP, 0, 0, tiled=...  6.03 us
  transfers between devices with their start and end apart: 4, of which 3 were waited for; matrix products, arithmetic and copies ran while one was open for 6% of the time, Pallas kernels for 0%

profile of v1, /device:TPU:8, one launch (start us, length us, event | category | flops | bytes accessed | tf_op | source)
XLA Modules:
  0.0 209.4 jit_solution(18382089865148208705)
XLA Ops:
  7.2 0.0 copy-start.4
  7.2 0.0 all-gather.4.cloned.1.call-start
  7.2 0.7 all-gather.4.cloned.1.call-update
  7.9 1.3 copy.25
  9.2 0.4 copy.19
  9.6 0.0 copy-done.4
  9.6 0.2 copy.20
  9.8 0.2 copy.21
  9.9 0.0 copy-start.5
  10.0 1.1 pad_maximum_fusion
  11.1 10.3 %all-to-all-start = ((bf16[8,576,128]{2,1,0:T(8,128)(2,1)}), bf16[8,576,128]{2,1,0:T(8,128)(2,1)S(1)}, u32[]{:S(2)}, u32[]{:S(2)}) async-start(bf16[8,576,128]{2,1,0:T(8,128)(2,1)} %pad_maximum_fusion), calls=%async_computation | async-start | bytes 2359296 | tf_op jit(solution)/shard_map/all_to_all | solution.py:36
  21.4 0.0 copy-done.5
  21.4 0.1 select_reduce_fusion
  21.5 0.1 fusion.11
  21.6 41.0 %all-to-all-done = bf16[8,576,128]{2,1,0:T(8,128)(2,1)S(1)} async-done(((bf16[8,576,128]{2,1,0:T(8,128)(2,1)}), bf16[8,576,128]{2,1,0:T(8,128)(2,1)S(1)}, u32[]{:S(2)}, u32[]{:S(2)}) %all-to-all-start) | async-done | bytes 1179680 | tf_op jit(solution)/shard_map/all_to_all | solution.py:36
  62.6 0.1 slice_reduce_fusion
  62.7 0.6 gather_fusion
  63.3 0.2 select_select_fusion
  63.5 22.4 %all_to_all.24 = bf16[64,16,128]{2,1,0:T(8,128)(2,1)S(1)} all-to-all(bf16[64,16,128]{2,1,0:T(8,128)(2,1)S(1)} %select_select_fusion), channel_id=1, replica_groups=mesh['fsdp_0'=4,'fsdp_1'=8,'fsdp_2'=2,'dp'=8] {'fsdp_0','fsdp_1','fsdp_2'}, dimensions={0} | all-to-all | bytes 524288 | tf_op jit(solution)/shard_map/all_to_all | solution.py:43
  85.9 0.0 all-gather.4.cloned.1.call-done
  85.9 1.6 tile.2
  87.5 3.6 %all-to-all-start.2 = ((bf16[1024,8,128]{2,0,1:T(8,128)(2,1)}), bf16[1024,8,128]{2,0,1:T(8,128)(2,1)S(1)}, u32[]{:S(2)}, u32[]{:S(2)}) async-start(bf16[1024,8,128]{2,0,1:T(8,128)(2,1)} %tile.2), calls=%async_computation.2 | async-start | bytes 4194304 | tf_op jit(solution)/shard_map/all_to_all | solution.py:52
  91.1 51.8 %all-to-all-done.2 = bf16[1024,8,128]{2,0,1:T(8,128)(2,1)S(1)} async-done(((bf16[1024,8,128]{2,0,1:T(8,128)(2,1)}), bf16[1024,8,128]{2,0,1:T(8,128)(2,1)S(1)}, u32[]{:S(2)}, u32[]{:S(2)}) %all-to-all-start.2) | async-done | bytes 2097184 | tf_op jit(solution)/shard_map/all_to_all | solution.py:52
  142.8 0.0 copy-start.1
  142.8 0.7 convolution_bitcast_fusion
  143.6 0.9 copy-done.1
  144.4 0.7 fusion.6
  145.1 1.3 fusion.14
  151.4 0.1 pad_maximum_fusion.2
  151.5 0.8 pad_maximum_fusion.1
  152.3 6.0 %all-to-all-start.3 = ((bf16[64,24,128]{2,1,0:T(8,128)(2,1)}), bf16[64,24,128]{2,1,0:T(8,128)(2,1)S(1)}, u32[]{:S(2)}, u32[]{:S(2)}) async-start(bf16[64,24,128]{2,1,0:T(8,128)(2,1)} %pad_maximum_fusion.1), calls=%async_computation.3 | async-start | bytes 786432 | tf_op jit(solution)/shard_map/all_to_all | solution.py:71
  158.4 0.0 copy-start.2
  158.4 2.6 %copy.22 = bf16[1024,8,128]{0,2,1:T(8,128)(2,1)} copy(bf16[1024,8,128]{2,0,1:T(8,128)(2,1)S(1)} %all-to-all-done.2) | data formatting | bytes 4194304 | tf_op jit(solution)/shard_map/all_to_all | solution.py:52
  161.0 0.0 copy-start
  161.0 0.0 copy-start.3
  161.0 0.0 copy-done.2
  161.0 3.1 %fusion.1 = f32[1,128,1024]{2,1,0:T(8,128)} fusion(f32[1,128,1024]{2,1,0:T(8,128)S(1)} %copy-done.2, bf16[1024,1024]{0,1:T(8,128)(2,1)} %bitcast.51, s32[]{:T(128)S(6)} %select_n.45), kind=kOutput, calls=%fused_computation.8 | convolution fusion | flops 268566528 | bytes 3407876 | tf_op jit(solution)/shard_map/rc,kc->rk/dot_general | solution.py:74
  164.1 0.0 copy-done
  164.1 0.0 copy-done.3
  164.1 1.6 fusion.2
  165.7 7.0 %all-to-all-done.3 = bf16[64,24,128]{2,1,0:T(8,128)(2,1)S(1)} async-done(((bf16[64,24,128]{2,1,0:T(8,128)(2,1)}), bf16[64,24,128]{2,1,0:T(8,128)(2,1)S(1)}, u32[]{:S(2)}, u32[]{:S(2)}) %all-to-all-start.3) | async-done | bytes 393248 | tf_op jit(solution)/shard_map/all_to_all | solution.py:71
  172.7 0.6 gather_fusion.1
  173.3 0.1 broadcast_select_fusion
  173.5 26.6 %all-gather.1 = bf16[3840,128]{1,0:T(8,128)(2,1)S(1)} all-gather(bf16[480,128]{1,0:T(8,128)(2,1)S(1)} %fusion.10), channel_id=3, replica_groups=mesh['fsdp_0'=4,'fsdp_1'=8,'fsdp_2'=2,'dp'=8] {'dp'}, dimensions={0}, use_global_device_ids=true | all-gather | bytes 1105920 | tf_op jit(solution)/shard_map/all_gather | solution.py:83
  200.2 0.1 slice.50
  200.2 0.1 convert_reduce_fusion
  200.4 0.3 fusion.3
  200.6 0.6 copy.23
  201.2 1.3 copy.29
  (13 shorter events, 0.1 us)
Async XLA Ops:
  7.2 2.4 %copy-start.4 = (bf16[1,128,1024]{2,1,0:T(8,128)(2,1)S(1)}, bf16[1,128,1024]{2,1,0:T(8,128)(2,1)}, u32[]{:S(2)}) copy-start(bf16[1,128,1024]{2,1,0:T(8,128)(2,1)} %param.13) | copy-start | bytes 786436
  7.2 78.7 %all-gather.4.cloned.1.call-start = ((), (), s32[]{:S(2)}) async-start(), calls=%async_computation.4 | async-start | bytes 2359296 | tf_op jit(solution)/shard_map/all_gather | solution.py:31
  9.9 11.4 %copy-start.5 = (s32[28]{0:T(128)S(1)}, s32[28]{0:T(128)}, u32[]{:S(2)}) copy-start(s32[28]{0:T(128)} %param.9) | copy-start | bytes 340
  11.1 51.5 %all-to-all-start = ((bf16[8,576,128]{2,1,0:T(8,128)(2,1)}), bf16[8,576,128]{2,1,0:T(8,128)(2,1)S(1)}, u32[]{:S(2)}, u32[]{:S(2)}) async-start(bf16[8,576,128]{2,1,0:T(8,128)(2,1)} %pad_maximum_fusion), calls=%async_computation | async-start | bytes 2359296 | tf_op jit(solution)/shard_map/all_to_all | solution.py:36
  87.5 55.4 %all-to-all-start.2 = ((bf16[1024,8,128]{2,0,1:T(8,128)(2,1)}), bf16[1024,8,128]{2,0,1:T(8,128)(2,1)S(1)}, u32[]{:S(2)}, u32[]{:S(2)}) async-start(bf16[1024,8,128]{2,0,1:T(8,128)(2,1)} %tile.2), calls=%async_computation.2 | async-start | bytes 4194304 | tf_op jit(solution)/shard_map/all_to_all | solution.py:52
  142.8 1.6 copy-start.1
  152.3 20.5 %all-to-all-start.3 = ((bf16[64,24,128]{2,1,0:T(8,128)(2,1)}), bf16[64,24,128]{2,1,0:T(8,128)(2,1)S(1)}, u32[]{:S(2)}, u32[]{:S(2)}) async-start(bf16[64,24,128]{2,1,0:T(8,128)(2,1)} %pad_maximum_fusion.1), calls=%async_computation.3 | async-start | bytes 786432 | tf_op jit(solution)/shard_map/all_to_all | solution.py:71
  158.4 2.6 %copy-start.2 = (f32[1,128,1024]{2,1,0:T(8,128)S(1)}, f32[1,128,1024]{2,1,0:T(8,128)}, u32[]{:S(2)}) copy-start(f32[1,128,1024]{2,1,0:T(8,128)} %param.10) | copy-start | bytes 1572868
  161.0 3.1 %copy-start = (bf16[1024,8,128]{0,2,1:T(8,128)(2,1)S(1)}, bf16[1024,8,128]{0,2,1:T(8,128)(2,1)}, u32[]{:S(2)}) copy-start(bf16[1024,8,128]{0,2,1:T(8,128)(2,1)} %copy.22) | copy-start | bytes 6291460
  161.0 3.1 %copy-start.3 = (f32[1,128,1024]{2,1,0:T(8,128)S(1)}, f32[1,128,1024]{2,1,0:T(8,128)}, u32[]{:S(2)}) copy-start(f32[1,128,1024]{2,1,0:T(8,128)} %param.11) | copy-start | bytes 1572868
Sparse Core Ops, SparseCore 0:
  10.1 63.5 all-gather.3
